TPU v7x, 32 devices: a whole 2x2x4 slice. The times are simulated.
32 devices in a mesh: row: 8 (over z, y), col: 4 (over x, core).
Axes of the slice: x: 2, y: 2, z: 4, core: 2. Of those that a mesh axis runs over, the one named last changes fastest.
Arguments:
- right_side: float32 [3, 64, 512], P(None, 'row', 'col'), may hold values from -6 to 6
- viscosity: float32 [64, 512], P('row', 'col'), may hold values from 0.1 to 3
- free_mask: int32 [3, 64, 512], P(None, 'row', 'col'), may hold values 0 or 1
- coarse_basis: float32 [64, 3, 64, 512], P(None, None, 'row', 'col'), may hold values from -6 to 6
- gram_inverse: float32 [64, 64], P('col'), may hold values from -3 to 6, as said below
Outputs:
- solution: float32 [3, 64, 512], P(None, 'row', 'col')
- residual: float32 [3, 64, 512], P(None, 'row', 'col')
Inputs may be any that keep to these rules, and one draw needn't show every extreme that they name: `free_mask`: 1 marks a free velocity unknown, 0 one whose value is prescribed. `gram_inverse`: symmetric positive definite.
All inputs are finite; a program needn't handle non-finite values. No bound on the sum of `free_mask` on one device may be relied on, other than what follows from the above.
Results may differ from a plain program's by a relative error of at most 0.0003.
Values sent between devices are 32-bit elements; how exact they have to be, the bound alone decides.
A program may use at most 64 MiB of HBM per device.

v0:
```python
import math
import jax
import jax.numpy as jnp
from jax import lax
from jax.sharding import PartitionSpec as P

ITERS = 2


def padded_2(shard, sides, width):
    for axis, dim in sides:
        count, length = (lax.axis_size(axis), shard.shape[dim])
        up = [(i, (i + 1) % count) for i in range(count - 1)]
        down = [(j, i) for i, j in up]
        last = lax.slice_in_dim(shard, length - width, length, axis=dim)
        leading = lax.slice_in_dim(shard, 0, width, axis=dim)
        before = lax.ppermute(last, axis, up)
        after = lax.ppermute(leading, axis, down)
        shard = jnp.concatenate([before, shard, after], axis=dim)
    return shard


def on_device(right_side, viscosity, free_mask, coarse_basis, gram_inverse):
    high = lax.Precision.HIGHEST
    components, patch_rows, patch_cols = right_side.shape
    columns = coarse_basis.shape[0]
    unknowns = (
        components * patch_rows * patch_cols * lax.axis_size("row") * lax.axis_size("col") * columns
    )
    coarse_scale = 1.0 / (32.0 * math.sqrt(float(unknowns)))
    viscosity_pad = padded_2(viscosity, (("row", 0), ("col", 1)), 1)
    face_north = 0.5 * (viscosity + viscosity_pad[2:, 1:-1])
    face_south = 0.5 * (viscosity + viscosity_pad[:-2, 1:-1])
    face_east = 0.5 * (viscosity + viscosity_pad[1:-1, 2:])
    face_west = 0.5 * (viscosity + viscosity_pad[1:-1, :-2])
    diagonal = 1.0 + face_north + face_south + face_east + face_west
    unfixed = free_mask.astype(jnp.float32)
    jacobi = unfixed / diagonal + (1.0 - unfixed)
    basis_rows = coarse_basis.reshape(columns, -1)

    def solve_coarse(coarse_dot):
        coeff_part = jnp.dot(gram_inverse, coarse_dot, precision=high) * coarse_scale
        return lax.all_gather(coeff_part, "col", axis=0, tiled=True)

    def precondition(residual, coarse_dot, weighted_sq):
        coeffs = solve_coarse(coarse_dot)
        smoothed = jacobi * residual + jnp.dot(coeffs, basis_rows, precision=high).reshape(
            residual.shape
        )
        return (smoothed, weighted_sq + jnp.dot(coarse_dot, coeffs, precision=high))

    solution = jnp.zeros_like(right_side)
    residual = right_side
    coarse_dot, weighted_sq = lax.psum(
        (
            jnp.dot(basis_rows, residual.reshape(-1), precision=high),
            jnp.sum(jacobi * residual * residual),
        ),
        ("row", "col"),
    )
    direction, energy = precondition(residual, coarse_dot, weighted_sq)
    for iteration in range(ITERS):
        masked = unfixed * direction
        padded = padded_2(masked, (("row", 1), ("col", 2)), 1)
        stencil = diagonal * masked - (
            face_north * padded[:, 2:, 1:-1]
            + face_south * padded[:, :-2, 1:-1]
            + face_east * padded[:, 1:-1, 2:]
            + face_west * padded[:, 1:-1, :-2]
        )
        applied = unfixed * stencil + (1.0 - unfixed) * direction
        if iteration + 1 < ITERS:
            curve_sum, image_coarse, cross_term, image_sq = lax.psum(
                (
                    jnp.sum(direction * applied),
                    jnp.dot(basis_rows, applied.reshape(-1), precision=high),
                    jnp.sum(jacobi * residual * applied),
                    jnp.sum(jacobi * applied * applied),
                ),
                ("row", "col"),
            )
            step_len = energy / curve_sum
            solution = step_len * direction
            residual = residual - step_len * applied
            coarse_dot = coarse_dot - step_len * image_coarse
            weighted_sq = weighted_sq - 2.0 * step_len * cross_term + step_len * step_len * image_sq
            smoothed, energy_new = precondition(residual, coarse_dot, weighted_sq)
            direction = smoothed + energy_new / energy * direction
            energy = energy_new
        else:
            curve_sum = lax.psum(jnp.sum(direction * applied), ("row", "col"))
            step_len = energy / curve_sum
            solution = solution + step_len * direction
            residual = residual - step_len * applied
    return (solution, residual)


def solution(mesh):
    in_specs = (
        P(None, "row", "col"),
        P("row", "col"),
        P(None, "row", "col"),
        P(None, None, "row", "col"),
        P("col", None),
    )
    out_specs = (P(None, "row", "col"), P(None, "row", "col"))
    return jax.shard_map(
        on_device, mesh=mesh, in_specs=in_specs, out_specs=out_specs, check_vma=False
    )
```

profile of v0, /device:TPU:0, one launch (start us, length us, event | category | flops | bytes accessed | tf_op | source)
XLA Modules:
  0.0 198.3 jit_solution(4688476039508117926)
XLA Ops:
  0.6 0.0 copy-start
  0.6 0.8 fusion.55
  1.4 1.3 collective-permute-start
  2.7 5.5 %collective-permute-start.1 = (f32[1,128]{1,0:T(1,128)S(1)}, f32[1,128]{1,0:T(1,128)S(1)}, u32[]{:S(2)}, u32[]{:S(2)}) collective-permute-start(f32[1,128]{1,0:T(1,128)S(1)} %get-tuple-element.33), channel_id=1, source_target_pairs={{0,4},{4,8},{8,12},{12,16},{16,20},{20,24},{24,28},{1,5},{5,9},{9,... | collective-permute-start | bytes 1544 | tf_op jit(solution)/shard_map/ppermute | solution.py:17
  8.2 1.3 copy.32
  9.5 0.0 copy-start.1
  9.5 0.0 copy-start.2
  9.5 0.1 copy.22
  9.7 1.0 copy-done.1
  10.7 0.0 copy-done.2
  10.7 0.7 convolution_bitcast_fusion.3
  11.4 41.9 %psum.50 = f32[64]{0:T(128)S(1)} all-reduce(f32[64]{0:T(128)S(1)} %convolution_bitcast_fusion.3), channel_id=1, replica_groups=mesh['row'=8,'col'=4] {'row','col'}, use_global_device_ids=true, to_apply=%region_2.0 | all-reduce | flops 64 | bytes 512 | tf_op jit(solution)/shard_map/psum | solution.py:54
  53.3 0.0 copy-done
  53.3 0.1 fusion.1
  53.4 0.0 copy-start.5
  53.4 0.7 copy-done.5
  54.1 0.6 dynamic-slice
  55.3 0.2 dynamic-update-slice
  55.5 5.8 %all-reduce = f32[64]{0:T(128)S(1)} all-reduce(f32[64]{0:T(128)S(1)} %dynamic-update-slice), channel_id=1, replica_groups=mesh['row'=8,'col'=4] {'col'}, use_global_device_ids=true, to_apply=%add | all-reduce | flops 64 | bytes 512
  61.3 0.0 copy-start.4
  61.3 0.6 fusion.4
  61.9 0.0 collective-permute-done
  61.9 0.0 collective-permute-done.1
  61.9 0.1 copy-done.4
  62.0 0.0 copy-start.3
  62.0 0.1 fusion.54
  62.1 1.3 collective-permute-start.2
  63.4 3.0 %collective-permute-start.3 = (f32[10,1]{1,0:T(8,128)S(1)}, f32[10,1]{1,0:T(8,128)S(1)}, u32[]{:S(2)}, u32[]{:S(2)}) collective-permute-start(f32[10,1]{1,0:T(8,128)S(1)} %get-tuple-element.31), channel_id=1, source_target_pairs={{0,1},{1,2},{2,3},{4,5},{5,6},{6,7},{8,9},{9,10},{10,11},{12,13},{... | collective-permute-start | bytes 128 | tf_op jit(solution)/shard_map/ppermute | solution.py:17
  66.4 0.0 collective-permute-done.2
  66.5 0.8 collective-permute-done.3
  67.3 0.1 add_add_fusion
  67.3 0.0 copy-done.3
  67.4 1.3 collective-permute-start.4
  68.7 4.8 %collective-permute-start.5 = (f32[3,1,128]{2,1,0:T(1,128)S(1)}, f32[3,1,128]{2,1,0:T(1,128)S(1)}, u32[]{:S(2)}, u32[]{:S(2)}) collective-permute-start(f32[3,1,128]{2,1,0:T(1,128)S(1)} %get-tuple-element.29), channel_id=1, source_target_pairs={{0,4},{4,8},{8,12},{12,16},{16,20},{20,24},{24,28},{1,5},{5,9},{9,... | collective-permute-start | bytes 4616 | tf_op jit(solution)/shard_map/ppermute | solution.py:17
  73.5 0.0 collective-permute-done.4
  73.5 1.3 collective-permute-done.5
  74.8 0.1 fusion.51
  74.9 2.3 %collective-permute-start.7 = (f32[3,10,1]{2,1,0:T(8,128)S(1)}, f32[3,10,1]{2,1,0:T(8,128)S(1)}, u32[]{:S(2)}, u32[]{:S(2)}) collective-permute-start(f32[3,10,1]{2,1,0:T(8,128)S(1)} %get-tuple-element.26), channel_id=1, source_target_pairs={{0,1},{1,2},{2,3},{4,5},{5,6},{6,7},{8,9},{9,10},{10,11},{12,13},{... | collective-permute-start | bytes 368 | tf_op jit(solution)/shard_map/ppermute | solution.py:17
  77.2 1.3 collective-permute-start.6
  78.5 0.7 multiply_reduce_fusion.5
  79.1 0.0 collective-permute-done.7
  79.1 4.0 %collective-permute-done.6 = f32[3,10,1]{2,1,0:T(8,128)S(1)} collective-permute-done((f32[3,10,1]{2,1,0:T(8,128)S(1)}, f32[3,10,1]{2,1,0:T(8,128)S(1)}, u32[]{:S(2)}, u32[]{:S(2)}) %collective-permute-start.6) | collective-permute-done | bytes 152 | tf_op jit(solution)/shard_map/ppermute | solution.py:18
  83.2 0.7 fusion.8
  83.9 0.7 convolution_bitcast_fusion.1
  84.6 42.6 %all-reduce.2 = (f32[64]{0:T(128)S(1)}, f32[]{:T(128)}, f32[]{:T(128)}, f32[]{:T(128)}, f32[]{:T(128)}) all-reduce(f32[64]{0:T(128)S(1)} %convolution_bitcast_fusion.1, f32[]{:T(128)} %get-tuple-element.4, f32[]{:T(128)} %get-tuple-element.5, f32[]{:T(128)} %get-tuple-element.3, ...), channel_id=1, replica_groups=mesh['row'=8,'col'=4] {'row','col'}, use_global_device_ids=true, to_apply=%region_9.0 | all-reduce | flops 68 | bytes 544 | tf_op jit(solution)/shard_map/psum | solution.py:73
  129.1 0.1 fusion
  129.2 0.2 dynamic-update-slice.1
  129.5 7.6 %all-reduce.1 = f32[64]{0:T(128)S(1)} all-reduce(f32[64]{0:T(128)S(1)} %dynamic-update-slice.1), channel_id=1, replica_groups=mesh['row'=8,'col'=4] {'col'}, use_global_device_ids=true, to_apply=%add.1 | all-reduce | flops 64 | bytes 512
  137.1 0.6 multiply_reduce_fusion.4
  137.7 0.6 fusion.2
  140.8 1.3 collective-permute-start.8
  142.1 4.5 %collective-permute-start.9 = (f32[3,1,128]{2,1,0:T(1,128)S(1)}, f32[3,1,128]{2,1,0:T(1,128)S(1)}, u32[]{:S(2)}, u32[]{:S(2)}) collective-permute-start(f32[3,1,128]{2,1,0:T(1,128)S(1)} %get-tuple-element.27), channel_id=1, source_target_pairs={{0,4},{4,8},{8,12},{12,16},{16,20},{20,24},{24,28},{1,5},{5,9},{9,... | collective-permute-start | bytes 4616 | tf_op jit(solution)/shard_map/ppermute | solution.py:17
  146.7 0.0 collective-permute-done.8
  146.7 1.3 collective-permute-done.9
  148.0 0.1 fusion.50
  148.0 1.3 collective-permute-start.11
  149.3 1.3 collective-permute-start.10
  150.6 0.0 collective-permute-done.11
  150.6 2.6 %collective-permute-done.10 = f32[3,10,1]{2,1,0:T(8,128)S(1)} collective-permute-done((f32[3,10,1]{2,1,0:T(8,128)S(1)}, f32[3,10,1]{2,1,0:T(8,128)S(1)}, u32[]{:S(2)}, u32[]{:S(2)}) %collective-permute-start.10) | collective-permute-done | bytes 152 | tf_op jit(solution)/shard_map/ppermute | solution.py:18
  153.3 0.7 multiply_reduce_fusion
  154.0 43.0 %psum.55 = f32[]{:T(128)} all-reduce(f32[]{:T(128)} %get-tuple-element.11), channel_id=1, replica_groups=mesh['row'=8,'col'=4] {'row','col'}, use_global_device_ids=true, to_apply=%region_11.0 | all-reduce | flops 1 | bytes 8 | tf_op jit(solution)/shard_map/psum | solution.py:91
  197.7 0.6 multiply_subtract_fusion
  (9 shorter events, 0.1 us)
Async XLA Ops:
  0.6 52.6 %copy-start = (f32[16,64]{1,0:T(8,128)S(1)}, f32[16,64]{1,0:T(8,128)}, u32[]{:S(2)}) copy-start(f32[16,64]{1,0:T(8,128)} %param.9) | copy-start | bytes 12292
  1.4 60.5 %collective-permute-start = (f32[1,128]{1,0:T(1,128)S(1)}, f32[1,128]{1,0:T(1,128)S(1)}, u32[]{:S(2)}, u32[]{:S(2)}) collective-permute-start(f32[1,128]{1,0:T(1,128)S(1)} %get-tuple-element.34), channel_id=1, source_target_pairs={{4,0},{8,4},{12,8},{16,12},{20,16},{24,20},{28,24},{5,1},{9,5},{13... | collective-permute-start | bytes 1544 | tf_op jit(solution)/shard_map/ppermute | solution.py:18
  2.7 59.2 %collective-permute-start.1 = (f32[1,128]{1,0:T(1,128)S(1)}, f32[1,128]{1,0:T(1,128)S(1)}, u32[]{:S(2)}, u32[]{:S(2)}) collective-permute-start(f32[1,128]{1,0:T(1,128)S(1)} %get-tuple-element.33), channel_id=1, source_target_pairs={{0,4},{4,8},{8,12},{12,16},{16,20},{20,24},{24,28},{1,5},{5,9},{9,... | collective-permute-start | bytes 1544 | tf_op jit(solution)/shard_map/ppermute | solution.py:17
  9.5 1.1 copy-start.1
  9.5 1.1 copy-start.2
  53.4 0.7 copy-start.5
  61.3 0.7 copy-start.4
  62.0 5.3 %copy-start.3 = (s32[3,8,128]{2,1,0:T(8,128)S(1)}, s32[3,8,128]{2,1,0:T(8,128)}, u32[]{:S(2)}) copy-start(s32[3,8,128]{2,1,0:T(8,128)} %param.7) | copy-start | bytes 36868
  62.1 4.3 %collective-permute-start.2 = (f32[10,1]{1,0:T(8,128)S(1)}, f32[10,1]{1,0:T(8,128)S(1)}, u32[]{:S(2)}, u32[]{:S(2)}) collective-permute-start(f32[10,1]{1,0:T(8,128)S(1)} %get-tuple-element.32), channel_id=1, source_target_pairs={{1,0},{2,1},{3,2},{5,4},{6,5},{7,6},{9,8},{10,9},{11,10},{13,12},{... | collective-permute-start | bytes 128 | tf_op jit(solution)/shard_map/ppermute | solution.py:18
  63.4 3.8 %collective-permute-start.3 = (f32[10,1]{1,0:T(8,128)S(1)}, f32[10,1]{1,0:T(8,128)S(1)}, u32[]{:S(2)}, u32[]{:S(2)}) collective-permute-start(f32[10,1]{1,0:T(8,128)S(1)} %get-tuple-element.31), channel_id=1, source_target_pairs={{0,1},{1,2},{2,3},{4,5},{5,6},{6,7},{8,9},{9,10},{10,11},{12,13},{... | collective-permute-start | bytes 128 | tf_op jit(solution)/shard_map/ppermute | solution.py:17
  67.4 6.1 %collective-permute-start.4 = (f32[3,1,128]{2,1,0:T(1,128)S(1)}, f32[3,1,128]{2,1,0:T(1,128)S(1)}, u32[]{:S(2)}, u32[]{:S(2)}) collective-permute-start(f32[3,1,128]{2,1,0:T(1,128)S(1)} %get-tuple-element.30), channel_id=1, source_target_pairs={{4,0},{8,4},{12,8},{16,12},{20,16},{24,20},{28,24},{5,1},{9,5},{13... | collective-permute-start | bytes 4616 | tf_op jit(solution)/shard_map/ppermute | solution.py:18
  68.7 6.1 %collective-permute-start.5 = (f32[3,1,128]{2,1,0:T(1,128)S(1)}, f32[3,1,128]{2,1,0:T(1,128)S(1)}, u32[]{:S(2)}, u32[]{:S(2)}) collective-permute-start(f32[3,1,128]{2,1,0:T(1,128)S(1)} %get-tuple-element.29), channel_id=1, source_target_pairs={{0,4},{4,8},{8,12},{12,16},{16,20},{20,24},{24,28},{1,5},{5,9},{9,... | collective-permute-start | bytes 4616 | tf_op jit(solution)/shard_map/ppermute | solution.py:17
  74.9 4.3 %collective-permute-start.7 = (f32[3,10,1]{2,1,0:T(8,128)S(1)}, f32[3,10,1]{2,1,0:T(8,128)S(1)}, u32[]{:S(2)}, u32[]{:S(2)}) collective-permute-start(f32[3,10,1]{2,1,0:T(8,128)S(1)} %get-tuple-element.26), channel_id=1, source_target_pairs={{0,1},{1,2},{2,3},{4,5},{5,6},{6,7},{8,9},{9,10},{10,11},{12,13},{... | collective-permute-start | bytes 368 | tf_op jit(solution)/shard_map/ppermute | solution.py:17
  77.2 6.0 %collective-permute-start.6 = (f32[3,10,1]{2,1,0:T(8,128)S(1)}, f32[3,10,1]{2,1,0:T(8,128)S(1)}, u32[]{:S(2)}, u32[]{:S(2)}) collective-permute-start(f32[3,10,1]{2,1,0:T(8,128)S(1)} %get-tuple-element.25), channel_id=1, source_target_pairs={{1,0},{2,1},{3,2},{5,4},{6,5},{7,6},{9,8},{10,9},{11,10},{13,12},{... | collective-permute-start | bytes 368 | tf_op jit(solution)/shard_map/ppermute | solution.py:18
  140.8 5.9 %collective-permute-start.8 = (f32[3,1,128]{2,1,0:T(1,128)S(1)}, f32[3,1,128]{2,1,0:T(1,128)S(1)}, u32[]{:S(2)}, u32[]{:S(2)}) collective-permute-start(f32[3,1,128]{2,1,0:T(1,128)S(1)} %get-tuple-element.28), channel_id=1, source_target_pairs={{4,0},{8,4},{12,8},{16,12},{20,16},{24,20},{28,24},{5,1},{9,5},{13... | collective-permute-start | bytes 4616 | tf_op jit(solution)/shard_map/ppermute | solution.py:18
  142.1 5.8 %collective-permute-start.9 = (f32[3,1,128]{2,1,0:T(1,128)S(1)}, f32[3,1,128]{2,1,0:T(1,128)S(1)}, u32[]{:S(2)}, u32[]{:S(2)}) collective-permute-start(f32[3,1,128]{2,1,0:T(1,128)S(1)} %get-tuple-element.27), channel_id=1, source_target_pairs={{0,4},{4,8},{8,12},{12,16},{16,20},{20,24},{24,28},{1,5},{5,9},{9,... | collective-permute-start | bytes 4616 | tf_op jit(solution)/shard_map/ppermute | solution.py:17
  148.0 2.6 %collective-permute-start.11 = (f32[3,10,1]{2,1,0:T(8,128)S(1)}, f32[3,10,1]{2,1,0:T(8,128)S(1)}, u32[]{:S(2)}, u32[]{:S(2)}) collective-permute-start(f32[3,10,1]{2,1,0:T(8,128)S(1)} %get-tuple-element.24), channel_id=1, source_target_pairs={{0,1},{1,2},{2,3},{4,5},{5,6},{6,7},{8,9},{9,10},{10,11},{12,13},{... | collective-permute-start | bytes 368 | tf_op jit(solution)/shard_map/ppermute | solution.py:17
  149.3 3.9 %collective-permute-start.10 = (f32[3,10,1]{2,1,0:T(8,128)S(1)}, f32[3,10,1]{2,1,0:T(8,128)S(1)}, u32[]{:S(2)}, u32[]{:S(2)}) collective-permute-start(f32[3,10,1]{2,1,0:T(8,128)S(1)} %get-tuple-element.23), channel_id=1, source_target_pairs={{1,0},{2,1},{3,2},{5,4},{6,5},{7,6},{9,8},{10,9},{11,10},{13,12},{... | collective-permute-start | bytes 368 | tf_op jit(solution)/shard_map/ppermute | solution.py:18
where the time goes:
time: 199 us; the launch traced here: 198 us
  blocking collectives  141 us (71%)
  starting transfers between devices  29.2 us (15%)
  waiting for transfers between devices  10 us (5%)
  between operations  6.67 us (3%)
  local copies, waits for them, and re-layouts  5.22 us (3%)
  other arithmetic  3.45 us (2%)
  matrix products  2.83 us (1%)
    psum x1, blocking collectives, on_device(): curve_sum = lax.psum(jnp.sum(direction * applied), ('row', 'col'))  43 us
    psum x1, blocking collectives, on_device(): lax.psum((jnp.sum(direction * applied), jnp.dot(basis_rows, applied.resha...  42.6 us
    psum x1, blocking collectives, on_device(): lax.psum((jnp.dot(basis_rows, residual.reshape(-1), precision=high), jnp....  41.9 us
    ppermute x6, starting transfers between devices, padded_2(): before = lax.ppermute(last, axis, up)  21.5 us
    unnamed x2, blocking collectives  13.4 us
    ppermute x6, starting transfers between devices, padded_2(): after = lax.ppermute(leading, axis, down)  7.73 us
    ppermute x6, waiting for transfers between devices, padded_2(): after = lax.ppermute(leading, axis, down)  6.67 us
    unnamed x19, local copies, waits for them, and re-layouts  4.22 us
  transfers between devices with their start and end apart: 12, of which 5 were waited for; matrix products, arithmetic and copies ran while one was open for 2% of the time, Pallas kernels for 0%

commit v1 on v0

--- a/solution.py
+++ b/solution.py
@@ -71,13 +71,16 @@
         applied = unfixed * stencil + (1.0 - unfixed) * direction
         if iteration + 1 < ITERS:
             curve_sum, image_coarse, cross_term, image_sq = lax.psum(
-                (
-                    jnp.sum(direction * applied),
-                    jnp.dot(basis_rows, applied.reshape(-1), precision=high),
-                    jnp.sum(jacobi * residual * applied),
-                    jnp.sum(jacobi * applied * applied),
+                lax.psum(
+                    (
+                        jnp.sum(direction * applied),
+                        jnp.dot(basis_rows, applied.reshape(-1), precision=high),
+                        jnp.sum(jacobi * residual * applied),
+                        jnp.sum(jacobi * applied * applied),
+                    ),
+                    "col",
                 ),
-                ("row", "col"),
+                "row",
             )
             step_len = energy / curve_sum
             solution = step_len * direction

time: 199 us -> 224 us (1.13)
  blocking collectives: 141 us -> 164 us
    psum x1 -> x2, blocking collectives: 41.9 us -> 84.3 us  [on_device(): lax.psum((jnp.dot(basis_rows, residual.reshape(-1), precision=high), jnp....]
    psum x1, blocking collectives: 42.6 us -> 8.39 us  [on_device(): lax.psum((jnp.sum(direction * applied), jnp.dot(basis_rows, applied.resha...]
    psum x0 -> x1, blocking collectives: none -> 19.3 us  [on_device(): lax.psum(lax.psum((jnp.sum(direction * applied), jnp.dot(basis_rows, appl...]
    psum x1, blocking collectives: 43 us -> 40.2 us  [on_device(): curve_sum = lax.psum(jnp.sum(direction * applied), ('row', 'col'))]
where the time goes in v1:
time: 224 us; the launch traced here: 223 us
  blocking collectives  164 us (73%)
  starting transfers between devices  29.2 us (13%)
  waiting for transfers between devices  11.6 us (5%)
  between operations  6.82 us (3%)
  local copies, waits for them, and re-layouts  5.22 us (2%)
  other arithmetic  3.44 us (2%)
  matrix products  2.83 us (1%)
    psum x2, blocking collectives, on_device(): lax.psum((jnp.dot(basis_rows, residual.reshape(-1), precision=high), jnp....  84.3 us
    psum x1, blocking collectives, on_device(): curve_sum = lax.psum(jnp.sum(direction * applied), ('row', 'col'))  40.2 us
    ppermute x6, starting transfers between devices, padded_2(): before = lax.ppermute(last, axis, up)  21.5 us
    psum x1, blocking collectives, on_device(): lax.psum(lax.psum((jnp.sum(direction * applied), jnp.dot(basis_rows, appl...  19.3 us
    unnamed x2, blocking collectives  11.4 us
    psum x1, blocking collectives, on_device(): lax.psum((jnp.sum(direction * applied), jnp.dot(basis_rows, applied.resha...  8.39 us
    ppermute x6, waiting for transfers between devices, padded_2(): after = lax.ppermute(leading, axis, down)  8.27 us
    ppermute x6, starting transfers between devices, padded_2(): after = lax.ppermute(leading, axis, down)  7.73 us
  transfers between devices with their start and end apart: 12, of which 5 were waited for; matrix products, arithmetic and copies ran while one was open for 2% of the time, Pallas kernels for 0%

profile of v1, /device:TPU:0, one launch (start us, length us, event | category | flops | bytes accessed | tf_op | source)
XLA Modules:
  0.0 222.7 jit_solution(1747593718300653777)
XLA Ops:
  0.6 0.0 copy-start
  0.6 0.8 fusion.55
  1.4 1.3 collective-permute-start
  2.7 5.5 %collective-permute-start.1 = (f32[1,128]{1,0:T(1,128)S(1)}, f32[1,128]{1,0:T(1,128)S(1)}, u32[]{:S(2)}, u32[]{:S(2)}) collective-permute-start(f32[1,128]{1,0:T(1,128)S(1)} %get-tuple-element.36), channel_id=1, source_target_pairs={{0,4},{4,8},{8,12},{12,16},{16,20},{20,24},{24,28},{1,5},{5,9},{9,... | collective-permute-start | bytes 1544 | tf_op jit(solution)/shard_map/ppermute | solution.py:17
  8.2 1.3 copy.32
  9.5 0.0 copy-start.1
  9.5 0.0 copy-start.2
  9.5 0.1 copy.22
  9.7 1.0 copy-done.1
  10.7 0.0 copy-done.2
  10.7 0.7 convolution_bitcast_fusion.3
  11.4 41.9 %psum.78 = f32[64]{0:T(128)S(1)} all-reduce(f32[64]{0:T(128)S(1)} %convolution_bitcast_fusion.3), channel_id=1, replica_groups=mesh['row'=8,'col'=4] {'row','col'}, use_global_device_ids=true, to_apply=%region_2.0 | all-reduce | flops 64 | bytes 512 | tf_op jit(solution)/shard_map/psum | solution.py:54
  53.3 0.0 copy-done
  53.3 0.1 fusion.1
  53.4 0.0 copy-start.5
  53.4 0.7 copy-done.5
  54.1 0.6 dynamic-slice
  55.3 0.2 dynamic-update-slice
  55.5 5.8 %all-reduce = f32[64]{0:T(128)S(1)} all-reduce(f32[64]{0:T(128)S(1)} %dynamic-update-slice), channel_id=1, replica_groups=mesh['row'=8,'col'=4] {'col'}, use_global_device_ids=true, to_apply=%add | all-reduce | flops 64 | bytes 512
  61.3 0.0 copy-start.4
  61.4 0.6 fusion.4
  61.9 0.0 collective-permute-done
  61.9 0.0 collective-permute-done.1
  61.9 0.1 copy-done.4
  62.0 0.0 copy-start.3
  62.1 0.1 fusion.54
  62.1 1.3 collective-permute-start.2
  63.4 3.0 %collective-permute-start.3 = (f32[10,1]{1,0:T(8,128)S(1)}, f32[10,1]{1,0:T(8,128)S(1)}, u32[]{:S(2)}, u32[]{:S(2)}) collective-permute-start(f32[10,1]{1,0:T(8,128)S(1)} %get-tuple-element.34), channel_id=1, source_target_pairs={{0,1},{1,2},{2,3},{4,5},{5,6},{6,7},{8,9},{9,10},{10,11},{12,13},{... | collective-permute-start | bytes 128 | tf_op jit(solution)/shard_map/ppermute | solution.py:17
  66.5 0.0 collective-permute-done.2
  66.5 0.8 collective-permute-done.3
  67.3 0.1 add_add_fusion
  67.3 0.0 copy-done.3
  67.4 1.3 collective-permute-start.4
  68.7 4.8 %collective-permute-start.5 = (f32[3,1,128]{2,1,0:T(1,128)S(1)}, f32[3,1,128]{2,1,0:T(1,128)S(1)}, u32[]{:S(2)}, u32[]{:S(2)}) collective-permute-start(f32[3,1,128]{2,1,0:T(1,128)S(1)} %get-tuple-element.32), channel_id=1, source_target_pairs={{0,4},{4,8},{8,12},{12,16},{16,20},{20,24},{24,28},{1,5},{5,9},{9,... | collective-permute-start | bytes 4616 | tf_op jit(solution)/shard_map/ppermute | solution.py:17
  73.5 0.0 collective-permute-done.4
  73.5 1.3 collective-permute-done.5
  74.8 0.1 fusion.51
  74.9 2.3 %collective-permute-start.7 = (f32[3,10,1]{2,1,0:T(8,128)S(1)}, f32[3,10,1]{2,1,0:T(8,128)S(1)}, u32[]{:S(2)}, u32[]{:S(2)}) collective-permute-start(f32[3,10,1]{2,1,0:T(8,128)S(1)} %get-tuple-element.29), channel_id=1, source_target_pairs={{0,1},{1,2},{2,3},{4,5},{5,6},{6,7},{8,9},{9,10},{10,11},{12,13},{... | collective-permute-start | bytes 368 | tf_op jit(solution)/shard_map/ppermute | solution.py:17
  77.2 1.3 collective-permute-start.6
  78.5 0.7 multiply_reduce_fusion.5
  79.1 0.0 collective-permute-done.7
  79.1 4.0 %collective-permute-done.6 = f32[3,10,1]{2,1,0:T(8,128)S(1)} collective-permute-done((f32[3,10,1]{2,1,0:T(8,128)S(1)}, f32[3,10,1]{2,1,0:T(8,128)S(1)}, u32[]{:S(2)}, u32[]{:S(2)}) %collective-permute-start.6) | collective-permute-done | bytes 152 | tf_op jit(solution)/shard_map/ppermute | solution.py:18
  83.2 0.7 fusion.8
  83.9 42.4 %psum.77 = f32[]{:T(128)} all-reduce(f32[]{:T(128)} %get-tuple-element.4), channel_id=1, replica_groups=mesh['row'=8,'col'=4] {'row','col'}, use_global_device_ids=true, to_apply=%region_1.0 | all-reduce | flops 1 | bytes 8 | tf_op jit(solution)/shard_map/psum | solution.py:54
  126.3 0.7 convolution_bitcast_fusion.1
  128.4 8.4 %all-reduce.3 = (f32[64]{0:T(128)S(1)}, f32[]{:T(128)}, f32[]{:T(128)}, f32[]{:T(128)}) all-reduce(f32[64]{0:T(128)S(1)} %convolution_bitcast_fusion.1, f32[]{:T(128)} %get-tuple-element.5, f32[]{:T(128)} %get-tuple-element.3, f32[]{:T(128)} %get-tuple-element.2), channel_id=1, replica_groups=mesh['row'=8,'col'=4] {'col'}, use_global_device_ids=true, to_apply=%region_12.0 | all-reduce | flops 67 | bytes 536 | tf_op jit(solution)/shard_map/psum | solution.py:74
  136.8 19.3 %all-reduce.2 = (f32[64]{0:T(128)S(1)}, f32[]{:T(128)}, f32[]{:T(128)}, f32[]{:T(128)}) all-reduce(f32[64]{0:T(128)S(1)} %get-tuple-element.10, f32[]{:T(128)} %get-tuple-element.11, f32[]{:T(128)} %get-tuple-element.12, f32[]{:T(128)} %get-tuple-element.13), channel_id=1, replica_groups=mesh['row'=8,'col'=4] {'row'}, use_global_device_ids=true, to_apply=%region_13.0 | all-reduce | flops 67 | bytes 536 | tf_op jit(solution)/shard_map/psum | solution.py:73
  156.6 0.1 fusion
  156.8 0.2 dynamic-update-slice.1
  157.0 5.6 %all-reduce.1 = f32[64]{0:T(128)S(1)} all-reduce(f32[64]{0:T(128)S(1)} %dynamic-update-slice.1), channel_id=1, replica_groups=mesh['row'=8,'col'=4] {'col'}, use_global_device_ids=true, to_apply=%add.1 | all-reduce | flops 64 | bytes 512
  162.6 0.6 multiply_reduce_fusion.4
  163.2 0.6 fusion.2
  166.5 1.3 collective-permute-start.8
  167.8 4.5 %collective-permute-start.9 = (f32[3,1,128]{2,1,0:T(1,128)S(1)}, f32[3,1,128]{2,1,0:T(1,128)S(1)}, u32[]{:S(2)}, u32[]{:S(2)}) collective-permute-start(f32[3,1,128]{2,1,0:T(1,128)S(1)} %get-tuple-element.30), channel_id=1, source_target_pairs={{0,4},{4,8},{8,12},{12,16},{16,20},{20,24},{24,28},{1,5},{5,9},{9,... | collective-permute-start | bytes 4616 | tf_op jit(solution)/shard_map/ppermute | solution.py:17
  172.3 0.0 collective-permute-done.8
  172.4 1.3 collective-permute-done.9
  173.6 0.1 fusion.50
  173.7 1.3 collective-permute-start.11
  175.0 1.3 collective-permute-start.10
  176.3 0.0 collective-permute-done.11
  176.3 4.2 %collective-permute-done.10 = f32[3,10,1]{2,1,0:T(8,128)S(1)} collective-permute-done((f32[3,10,1]{2,1,0:T(8,128)S(1)}, f32[3,10,1]{2,1,0:T(8,128)S(1)}, u32[]{:S(2)}, u32[]{:S(2)}) %collective-permute-start.10) | collective-permute-done | bytes 152 | tf_op jit(solution)/shard_map/ppermute | solution.py:18
  180.5 0.7 multiply_reduce_fusion
  181.2 40.2 %psum.87 = f32[]{:T(128)} all-reduce(f32[]{:T(128)} %get-tuple-element.14), channel_id=1, replica_groups=mesh['row'=8,'col'=4] {'row','col'}, use_global_device_ids=true, to_apply=%region_15.0 | all-reduce | flops 1 | bytes 8 | tf_op jit(solution)/shard_map/psum | solution.py:94
  222.1 0.6 multiply_subtract_fusion
  (9 shorter events, 0.1 us)
Async XLA Ops:
  0.6 52.6 %copy-start = (f32[16,64]{1,0:T(8,128)S(1)}, f32[16,64]{1,0:T(8,128)}, u32[]{:S(2)}) copy-start(f32[16,64]{1,0:T(8,128)} %param.9) | copy-start | bytes 12292
  1.4 60.5 %collective-permute-start = (f32[1,128]{1,0:T(1,128)S(1)}, f32[1,128]{1,0:T(1,128)S(1)}, u32[]{:S(2)}, u32[]{:S(2)}) collective-permute-start(f32[1,128]{1,0:T(1,128)S(1)} %get-tuple-element.37), channel_id=1, source_target_pairs={{4,0},{8,4},{12,8},{16,12},{20,16},{24,20},{28,24},{5,1},{9,5},{13... | collective-permute-start | bytes 1544 | tf_op jit(solution)/shard_map/ppermute | solution.py:18
  2.7 59.2 %collective-permute-start.1 = (f32[1,128]{1,0:T(1,128)S(1)}, f32[1,128]{1,0:T(1,128)S(1)}, u32[]{:S(2)}, u32[]{:S(2)}) collective-permute-start(f32[1,128]{1,0:T(1,128)S(1)} %get-tuple-element.36), channel_id=1, source_target_pairs={{0,4},{4,8},{8,12},{12,16},{16,20},{20,24},{24,28},{1,5},{5,9},{9,... | collective-permute-start | bytes 1544 | tf_op jit(solution)/shard_map/ppermute | solution.py:17
  9.5 1.1 copy-start.1
  9.5 1.1 copy-start.2
  53.4 0.7 copy-start.5
  61.3 0.7 copy-start.4
  62.0 5.3 %copy-start.3 = (s32[3,8,128]{2,1,0:T(8,128)S(1)}, s32[3,8,128]{2,1,0:T(8,128)}, u32[]{:S(2)}) copy-start(s32[3,8,128]{2,1,0:T(8,128)} %param.7) | copy-start | bytes 36868
  62.1 4.3 %collective-permute-start.2 = (f32[10,1]{1,0:T(8,128)S(1)}, f32[10,1]{1,0:T(8,128)S(1)}, u32[]{:S(2)}, u32[]{:S(2)}) collective-permute-start(f32[10,1]{1,0:T(8,128)S(1)} %get-tuple-element.35), channel_id=1, source_target_pairs={{1,0},{2,1},{3,2},{5,4},{6,5},{7,6},{9,8},{10,9},{11,10},{13,12},{... | collective-permute-start | bytes 128 | tf_op jit(solution)/shard_map/ppermute | solution.py:18
  63.4 3.8 %collective-permute-start.3 = (f32[10,1]{1,0:T(8,128)S(1)}, f32[10,1]{1,0:T(8,128)S(1)}, u32[]{:S(2)}, u32[]{:S(2)}) collective-permute-start(f32[10,1]{1,0:T(8,128)S(1)} %get-tuple-element.34), channel_id=1, source_target_pairs={{0,1},{1,2},{2,3},{4,5},{5,6},{6,7},{8,9},{9,10},{10,11},{12,13},{... | collective-permute-start | bytes 128 | tf_op jit(solution)/shard_map/ppermute | solution.py:17
  67.4 6.1 %collective-permute-start.4 = (f32[3,1,128]{2,1,0:T(1,128)S(1)}, f32[3,1,128]{2,1,0:T(1,128)S(1)}, u32[]{:S(2)}, u32[]{:S(2)}) collective-permute-start(f32[3,1,128]{2,1,0:T(1,128)S(1)} %get-tuple-element.33), channel_id=1, source_target_pairs={{4,0},{8,4},{12,8},{16,12},{20,16},{24,20},{28,24},{5,1},{9,5},{13... | collective-permute-start | bytes 4616 | tf_op jit(solution)/shard_map/ppermute | solution.py:18
  68.7 6.1 %collective-permute-start.5 = (f32[3,1,128]{2,1,0:T(1,128)S(1)}, f32[3,1,128]{2,1,0:T(1,128)S(1)}, u32[]{:S(2)}, u32[]{:S(2)}) collective-permute-start(f32[3,1,128]{2,1,0:T(1,128)S(1)} %get-tuple-element.32), channel_id=1, source_target_pairs={{0,4},{4,8},{8,12},{12,16},{16,20},{20,24},{24,28},{1,5},{5,9},{9,... | collective-permute-start | bytes 4616 | tf_op jit(solution)/shard_map/ppermute | solution.py:17
  74.9 4.3 %collective-permute-start.7 = (f32[3,10,1]{2,1,0:T(8,128)S(1)}, f32[3,10,1]{2,1,0:T(8,128)S(1)}, u32[]{:S(2)}, u32[]{:S(2)}) collective-permute-start(f32[3,10,1]{2,1,0:T(8,128)S(1)} %get-tuple-element.29), channel_id=1, source_target_pairs={{0,1},{1,2},{2,3},{4,5},{5,6},{6,7},{8,9},{9,10},{10,11},{12,13},{... | collective-permute-start | bytes 368 | tf_op jit(solution)/shard_map/ppermute | solution.py:17
  77.2 6.0 %collective-permute-start.6 = (f32[3,10,1]{2,1,0:T(8,128)S(1)}, f32[3,10,1]{2,1,0:T(8,128)S(1)}, u32[]{:S(2)}, u32[]{:S(2)}) collective-permute-start(f32[3,10,1]{2,1,0:T(8,128)S(1)} %get-tuple-element.28), channel_id=1, source_target_pairs={{1,0},{2,1},{3,2},{5,4},{6,5},{7,6},{9,8},{10,9},{11,10},{13,12},{... | collective-permute-start | bytes 368 | tf_op jit(solution)/shard_map/ppermute | solution.py:18
  166.5 5.9 %collective-permute-start.8 = (f32[3,1,128]{2,1,0:T(1,128)S(1)}, f32[3,1,128]{2,1,0:T(1,128)S(1)}, u32[]{:S(2)}, u32[]{:S(2)}) collective-permute-start(f32[3,1,128]{2,1,0:T(1,128)S(1)} %get-tuple-element.31), channel_id=1, source_target_pairs={{4,0},{8,4},{12,8},{16,12},{20,16},{24,20},{28,24},{5,1},{9,5},{13... | collective-permute-start | bytes 4616 | tf_op jit(solution)/shard_map/ppermute | solution.py:18
  167.8 5.8 %collective-permute-start.9 = (f32[3,1,128]{2,1,0:T(1,128)S(1)}, f32[3,1,128]{2,1,0:T(1,128)S(1)}, u32[]{:S(2)}, u32[]{:S(2)}) collective-permute-start(f32[3,1,128]{2,1,0:T(1,128)S(1)} %get-tuple-element.30), channel_id=1, source_target_pairs={{0,4},{4,8},{8,12},{12,16},{16,20},{20,24},{24,28},{1,5},{5,9},{9,... | collective-permute-start | bytes 4616 | tf_op jit(solution)/shard_map/ppermute | solution.py:17
  173.7 2.6 %collective-permute-start.11 = (f32[3,10,1]{2,1,0:T(8,128)S(1)}, f32[3,10,1]{2,1,0:T(8,128)S(1)}, u32[]{:S(2)}, u32[]{:S(2)}) collective-permute-start(f32[3,10,1]{2,1,0:T(8,128)S(1)} %get-tuple-element.27), channel_id=1, source_target_pairs={{0,1},{1,2},{2,3},{4,5},{5,6},{6,7},{8,9},{9,10},{10,11},{12,13},{... | collective-permute-start | bytes 368 | tf_op jit(solution)/shard_map/ppermute | solution.py:17
  175.0 5.5 %collective-permute-start.10 = (f32[3,10,1]{2,1,0:T(8,128)S(1)}, f32[3,10,1]{2,1,0:T(8,128)S(1)}, u32[]{:S(2)}, u32[]{:S(2)}) collective-permute-start(f32[3,10,1]{2,1,0:T(8,128)S(1)} %get-tuple-element.26), channel_id=1, source_target_pairs={{1,0},{2,1},{3,2},{5,4},{6,5},{7,6},{9,8},{10,9},{11,10},{13,12},{... | collective-permute-start | bytes 368 | tf_op jit(solution)/shard_map/ppermute | solution.py:18
